TPU v7x, 32 devices: a whole 2x2x4 slice. The times are simulated.
32 devices in a mesh: net: 4 (over y, x), line: 8 (over z, core).
Axes of the slice: x: 2, y: 2, z: 4, core: 2. Of those that a mesh axis runs over, the one named last changes fastest.
Arguments:
- conductance_inverse: float32 [4, 4096, 4096], P('net', 'line'), may hold values from -0.5 to 4.5, as said below
- prior_voltage: float32 [4, 96, 4096], P('net', None, 'line'), may hold values from -6 to 6
- sources: float32 [3, 4, 4096], P(None, 'net', 'line'), may hold values from -6 to 6
- fault_node: int32 [96], replicated, may hold values from 0 to 16383
- fault_conductance: float32 [96], replicated, may hold values from 0.5 to 4
- terminal_node: int32 [4, 3, 4096], P('net', None, 'line'), may hold values from 0 to 4095
- ownership: int32 [4, 4096], P('net', 'line'), may hold values from 0 to 1, as said below
- partner: int32 [4, 4096], P('net', 'line'), may hold values from 0 to 31, as said below
- delay_steps: int32 [4, 4096], P('net', 'line'), may hold values from 1 to 4, as said below
- surge_conductance: float32 [4, 4096], P('net', 'line'), may hold values from 0.2 to 1
- pole_wave: float32 [4, 6, 4096], P('net', None, 'line'), may hold values from 0.2 to 0.95
- residue_wave: float32 [4, 6, 3, 3, 4096], P('net', None, None, None, 'line'), may hold values from -1 to 1
- pole_admit: float32 [4, 6, 4096], P('net', None, 'line'), may hold values from 0.2 to 0.95
- residue_admit: float32 [4, 6, 3, 3, 4096], P('net', None, None, None, 'line'), may hold values from -1 to 1
- wave_state: float32 [4, 6, 3, 96, 4096], P('net', None, None, None, 'line'), may hold values from -4 to 4
- admit_state: float32 [4, 6, 3, 96, 4096], P('net', None, None, None, 'line'), may hold values from -4 to 4
- wave_history: float32 [4, 4, 3, 96, 4096], P('net', None, None, None, 'line'), may hold values from -6 to 6
Outputs:
- final_voltage: float32 [4, 96, 4096], P('net', None, 'line')
- end_current: float32 [4, 3, 96, 4096], P('net', None, None, 'line')
Inputs may be any that keep to these rules, and one draw needn't show every extreme that they name: `conductance_inverse`: each block is exactly symmetric. `ownership`: A slot is live exactly when the slot of the same number j % 512 at its partner owner is live; the number of live slots differs from owner to owner. The far end of slot j lies in the slot of the same number j % 512 at the partner owner, the partner of that slot is the first owner again, never the owner itself, and at most 17 live slots of one owner have the same partner; this many occur. `delay_steps`: equal at both ends of a line.
All inputs are finite; a program needn't handle non-finite values.
Results may differ from a plain program's by a relative error of at most 0.0003.
Values sent between devices are 32-bit elements; how exact they have to be, the bound alone decides.
A program may use at most 128 MiB of HBM per device.

v0:
```python
import jax
import jax.numpy as jnp
from jax import lax
from jax.sharding import PartitionSpec as P

STEPS = 3


def mix_residue(residue, vector):
    return (
        residue[:, :, 0, None, :] * vector[0]
        + residue[:, :, 1, None, :] * vector[1]
        + residue[:, :, 2, None, :] * vector[2]
    )


def select_delayed(buffer, delay_local):
    depth_count = buffer.shape[0]
    chosen = delay_local[None, :] == jnp.arange(1, depth_count + 1, dtype=jnp.int32)[:, None]
    return jnp.sum(jnp.where(chosen[:, None, None, :], buffer, 0.0), axis=0)


def terminal_values(voltage, terminal):
    picked = jnp.take(voltage, terminal.reshape(-1), axis=1)
    return jnp.moveaxis(picked.reshape(voltage.shape[0], 3, -1), 0, 1)


def spread_ends(history, terminal, node_count):
    values = jnp.moveaxis(history, 0, 1).reshape(history.shape[1], -1)
    return (
        jnp.zeros((history.shape[1], node_count), jnp.float32)
        .at[:, terminal.reshape(-1)]
        .add(values)
    )


def gather_full(block):
    return lax.all_gather(block, "line", axis=1, tiled=True)


def on_device(
    conductance_inverse,
    prior_voltage,
    sources,
    fault_node,
    fault_conductance,
    terminal_node,
    ownership,
    partner,
    delay_steps,
    surge_conductance,
    pole_wave,
    residue_wave,
    pole_admit,
    residue_admit,
    wave_state,
    admit_state,
    wave_history,
):
    inverse_block = conductance_inverse[0]
    row_count = inverse_block.shape[0]
    node_count = inverse_block.shape[1]
    line_index = lax.axis_index("line")
    net_index = lax.axis_index("net")
    offset = line_index * row_count
    net_count = lax.axis_size("net")
    line_count = lax.axis_size("line")
    devices = net_count * line_count
    slot_count = ownership.shape[1]
    capacity = (slot_count + devices - 2) // (devices - 1)
    is_live = ownership[0] > 0
    live_float = is_live.astype(jnp.float32)
    terminal = terminal_node[0]
    delay_local = delay_steps[0]
    surge_local = surge_conductance[0]
    partners = partner[0]
    slot_range = jnp.arange(slot_count, dtype=jnp.int32)
    earlier = (
        (partners[:, None] == partners[None, :])
        & is_live[None, :]
        & (slot_range[None, :] < slot_range[:, None])
    )
    slot_rank = jnp.sum(earlier.astype(jnp.int32), axis=1)
    position = jnp.where(is_live, partners * capacity + slot_rank, devices * capacity)
    scenario_range = jnp.arange(prior_voltage.shape[1], dtype=jnp.int32)
    fault_sub = fault_node // node_count
    fault_local = fault_node % node_count
    fault_here = (fault_sub == net_index) & (fault_local // row_count == line_index)
    wave_decay = pole_wave[0][:, None, None, :]
    admit_decay = pole_admit[0][:, None, None, :]
    wave_res = residue_wave[0]
    admit_res = residue_admit[0]
    voltage = gather_full(prior_voltage[0])
    voltage_rows = prior_voltage[0]
    wave_now = wave_state[0]
    admits = admit_state[0]
    history_buffer = wave_history[0]
    outgoing = None
    current = None
    for step_index in range(STEPS):
        terminal_prior = terminal_values(voltage, terminal)
        admits = admit_decay * admits + mix_residue(admit_res, terminal_prior)
        if step_index == 0:
            wave_now = wave_decay * wave_now + mix_residue(
                wave_res, select_delayed(history_buffer, delay_local)
            )
        else:
            shifted = jnp.concatenate(
                [jnp.zeros_like(history_buffer[:1]), history_buffer[:-1]], axis=0
            )
            wave_now = wave_decay * wave_now + mix_residue(
                wave_res, select_delayed(shifted, delay_local)
            )
            row_width = outgoing.shape[0] * outgoing.shape[1]
            packed = jnp.moveaxis(outgoing, 2, 0).reshape(slot_count, row_width)
            buffer = (
                jnp.zeros((devices * capacity, row_width), jnp.float32)
                .at[position]
                .set(packed, mode="drop")
            )
            arrived = lax.all_to_all(
                buffer, ("net", "line"), split_axis=0, concat_axis=0, tiled=True
            )
            picked_rows = arrived[jnp.minimum(position, devices * capacity - 1)]
            arrived = jnp.moveaxis(picked_rows.reshape(slot_count, 3, -1), 0, 2) * live_float
            newest = jnp.where((delay_local == 1)[None, None, :], arrived, 0.0)
            wave_now = wave_now + mix_residue(wave_res, newest)
            history_buffer = jnp.concatenate([arrived[None], shifted[1:]], axis=0)
        history = (jnp.sum(wave_now, axis=0) - jnp.sum(admits, axis=0)) * live_float
        injection = spread_ends(history, terminal, node_count)
        own_part = (
            lax.dynamic_slice_in_dim(injection, offset, row_count, 1)
            + sources[step_index, 0][None, :]
        )
        injection = lax.dynamic_update_slice_in_dim(injection, own_part, offset, 1)
        fault_value = voltage[scenario_range, fault_local]
        injection = injection.at[scenario_range, fault_local].add(
            jnp.where(fault_here, -fault_conductance * fault_value, 0.0)
        )
        summed = lax.psum(injection, "line")
        voltage_rows = lax.dot_general(
            summed,
            inverse_block,
            (((1,), (1,)), ((), ())),
            precision=lax.Precision.HIGHEST,
            preferred_element_type=jnp.float32,
        )
        voltage = gather_full(voltage_rows)
        terminal_now = terminal_values(voltage, terminal)
        if step_index + 1 < STEPS:
            outgoing = (2.0 * surge_local * terminal_now - history) * live_float
        else:
            current = (surge_local * terminal_now - history) * live_float
    return (voltage_rows[None], current[None])


def solution(mesh):
    return jax.shard_map(
        on_device,
        mesh=mesh,
        in_specs=(
            P("net", "line", None),
            P("net", None, "line"),
            P(None, "net", "line"),
            P(),
            P(),
            P("net", None, "line"),
            P("net", "line"),
            P("net", "line"),
            P("net", "line"),
            P("net", "line"),
            P("net", None, "line"),
            P("net", None, None, None, "line"),
            P("net", None, "line"),
            P("net", None, None, None, "line"),
            P("net", None, None, None, "line"),
            P("net", None, None, None, "line"),
            P("net", None, None, None, "line"),
        ),
        out_specs=(P("net", None, "line"), P("net", None, None, "line")),
        check_vma=False,
    )
```

profile of v0, /device:TPU:0, one launch (start us, length us, event | category | flops | bytes accessed | tf_op | source)
XLA Modules:
  0.0 577.8 jit_solution(13432879487147559588)
XLA Ops:
  32.9 8.7 %all-gather.12.cloned.1.call-done = f32[1,96,4096]{1,2,0:T(8,128)} async-done(((f32[1,96,512]{1,2,0:T(8,128)}), f32[1,96,4096]{1,2,0:T(8,128)}) %all-gather.12.cloned.1.call-update) | async-done | bytes 1572880 | tf_op jit(solution)/shard_map/all_gather | solution.py:38
  45.1 5.6 gather_fusion.5
  64.7 10.5 %scatter_custom_fusion = f32[96,4096]{0,1:T(8,128)} fusion(s32[1536]{0:T(1024)} %fusion.32, f32[1536,96]{1,0:T(8,128)} %copy.74, f32[]{:T(128)} %constant.37.clone.1), kind=kCustom, calls=%fused_computation.47 | custom fusion | flops 147456 | bytes 1573376 | tf_op jit(solution)/shard_map/scatter-add | solution.py:33
  81.1 12.2 %scatter_fusion = f32[96,4096]{1,0:T(8,128)} fusion(f32[96,4096]{1,0:T(8,128)} %copy.75, s32[96]{0:T(128)S(1)} %fusion.36, f32[96]{0:T(128)} %get-tuple-element.9), kind=kCustom, calls=%fused_computation.10 | custom fusion | flops 96 | bytes 1920 | tf_op jit(solution)/shard_map/scatter-add | solution.py:137
  93.6 61.2 %all-reduce.6.cloned.1.call-done = f32[96,4096]{1,0:T(8,128)} async-done(((f32[96,4096]{1,0:T(8,128)}), f32[96,4096]{1,0:T(8,128)}) %all-reduce.6.cloned.1.call-update) | async-done | bytes 1572880 | tf_op jit(solution)/shard_map/psum | solution.py:140
  154.8 12.7 %fusion.4 = f32[96,512]{1,0:T(8,128)} fusion(f32[96,4096]{1,0:T(8,128)} %all-reduce.6.cloned.1.call-done, f32[1,512,4096]{2,1,0:T(8,128)} %param.19), kind=kOutput, calls=%fused_computation.21 | convolution fusion | flops 2415919104 | bytes 10158080 | tf_op jit(solution)/shard_map/dot_general | solution.py:141
  174.4 17.7 %all-gather.6.cloned.1.call-done = f32[96,4096]{1,0:T(8,128)} async-done(((f32[96,512]{1,0:T(8,128)}), f32[96,4096]{1,0:T(8,128)}) %all-gather.6.cloned.1.call-update) | async-done | bytes 1572880 | tf_op jit(solution)/shard_map/all_gather | solution.py:38
  194.9 5.6 gather_fusion.6
  215.7 3.8 all-to-all-start
  234.3 4.2 fusion.11
  238.5 11.3 %all-to-all-done = f32[32,17,288]{2,1,0:T(8,128)} async-done(((f32[32,17,288]{2,1,0:T(8,128)}), f32[32,17,288]{2,1,0:T(8,128)}, u32[]{:S(2)}, u32[]{:S(2)}) %all-to-all-start) | async-done | bytes 626720 | tf_op jit(solution)/shard_map/all_to_all | solution.py:121
  256.8 3.9 fusion.38
  262.1 9.4 %scatter_custom_fusion.3 = f32[96,4096]{0,1:T(8,128)S(1)} fusion(s32[1536]{0:T(1024)} %fusion.32, f32[1536,96]{1,0:T(8,128)S(1)} %copy.84, f32[]{:T(128)} %constant.37.clone.1), kind=kCustom, calls=%fused_computation.45 | custom fusion | flops 147456 | bytes 1573376 | tf_op jit(solution)/shard_map/scatter-add | solution.py:33
  273.3 12.2 %scatter_fusion.1 = f32[96,4096]{1,0:T(8,128)} fusion(f32[96,4096]{1,0:T(8,128)} %copy.85, s32[96]{0:T(128)S(1)} %fusion.36, f32[96]{0:T(128)S(1)} %copy-done.45), kind=kCustom, calls=%fused_computation.13 | custom fusion | flops 96 | bytes 1920 | tf_op jit(solution)/shard_map/scatter-add | solution.py:137
  286.0 59.3 %all-reduce.8.cloned.1.call-done = f32[96,4096]{1,0:T(8,128)} async-done(((f32[96,4096]{1,0:T(8,128)}), f32[96,4096]{1,0:T(8,128)}) %all-reduce.8.cloned.1.call-update) | async-done | bytes 1572880 | tf_op jit(solution)/shard_map/psum | solution.py:140
  345.3 12.6 %fusion.2 = f32[96,512]{1,0:T(8,128)} fusion(f32[96,4096]{1,0:T(8,128)} %all-reduce.8.cloned.1.call-done, f32[1,512,4096]{2,1,0:T(8,128)} %param.19), kind=kOutput, calls=%fused_computation.19 | convolution fusion | flops 2415919104 | bytes 10158080 | tf_op jit(solution)/shard_map/dot_general | solution.py:141
  358.8 23.8 %all-gather.8.cloned.1.call-done = f32[96,4096]{1,0:T(8,128)} async-done(((f32[96,512]{1,0:T(8,128)}), f32[96,4096]{1,0:T(8,128)}) %all-gather.8.cloned.1.call-update) | async-done | bytes 1572880 | tf_op jit(solution)/shard_map/all_gather | solution.py:38
  412.3 4.8 add_reduce_fusion
  417.2 13.2 %all-to-all-done.1 = f32[32,17,288]{2,1,0:T(8,128)} async-done(((f32[32,17,288]{2,1,0:T(8,128)}), f32[32,17,288]{2,1,0:T(8,128)}, u32[]{:S(2)}, u32[]{:S(2)}) %all-to-all-start.1) | async-done | bytes 626720 | tf_op jit(solution)/shard_map/all_to_all | solution.py:121
  442.0 9.4 %scatter_custom_fusion.6 = f32[96,4096]{0,1:T(8,128)S(1)} fusion(s32[1536]{0:T(1024)} %fusion.32, f32[1536,96]{1,0:T(8,128)S(1)} %copy.94, f32[]{:T(128)} %constant.37.clone.1), kind=kCustom, calls=%fused_computation.43 | custom fusion | flops 147456 | bytes 1573376 | tf_op jit(solution)/shard_map/scatter-add | solution.py:33
  453.2 12.2 %scatter_fusion.2 = f32[96,4096]{1,0:T(8,128)} fusion(f32[96,4096]{1,0:T(8,128)} %copy.95, s32[96]{0:T(128)S(1)} %fusion.36, f32[96]{0:T(128)S(1)} %copy-done.44), kind=kCustom, calls=%fused_computation.16 | custom fusion | flops 96 | bytes 1920 | tf_op jit(solution)/shard_map/scatter-add | solution.py:137
  465.7 59.5 %all-reduce.10.cloned.1.call-done = f32[96,4096]{1,0:T(8,128)} async-done(((f32[96,4096]{1,0:T(8,128)}), f32[96,4096]{1,0:T(8,128)}) %all-reduce.10.cloned.1.call-update) | async-done | bytes 1572880 | tf_op jit(solution)/shard_map/psum | solution.py:140
  525.2 12.7 %fusion = f32[96,512]{1,0:T(8,128)} fusion(f32[96,4096]{1,0:T(8,128)} %all-reduce.10.cloned.1.call-done, f32[1,512,4096]{2,1,0:T(8,128)} %param.19), kind=kOutput, calls=%fused_computation.17 | convolution fusion | flops 2415919104 | bytes 10158080 | tf_op jit(solution)/shard_map/dot_general | solution.py:141
  537.9 24.6 %all-gather.10.cloned.1.call-done = f32[96,4096]{1,0:T(8,128)} async-done(((f32[96,512]{1,0:T(8,128)}), f32[96,4096]{1,0:T(8,128)}) %all-gather.10.cloned.1.call-update) | async-done | bytes 1572880 | tf_op jit(solution)/shard_map/all_gather | solution.py:38
  (215 shorter events, 151.6 us)
Async XLA Ops:
  7.2 18.5 %copy-start.46 = (s32[96]{0:T(128)S(1)}, s32[96]{0:T(128)}, u32[]{:S(2)}) copy-start(s32[96]{0:T(128)} %param.22) | copy-start | bytes 1156
  7.2 23.8 %copy-start.2 = (f32[1,6,3,96,512]{4,3,2,1,0:T(8,128)S(1)}, f32[1,6,3,96,512]{4,3,2,1,0:T(8,128)}, u32[]{:S(2)}) copy-start(f32[1,6,3,96,512]{4,3,2,1,0:T(8,128)} %param.33) | copy-start | bytes 10616836
  7.2 34.3 %all-gather.12.cloned.1.call-start = ((), (), s32[]{:S(2)}) async-start(), calls=%async_computation.8 | async-start | bytes 2359296 | tf_op jit(solution)/shard_map/all_gather | solution.py:38
  9.2 145.6 %all-reduce.6.cloned.1.call-start = ((), (), s32[]{:S(2)}) async-start(), calls=%async_computation.2 | async-start | bytes 3145728 | tf_op jit(solution)/shard_map/psum | solution.py:140
  12.5 11.2 %copy-start.35 = (s32[1536]{0:T(1024)}, s32[1536]{0:T(1024)S(1)}, u32[]{:S(2)}) copy-start(s32[1536]{0:T(1024)S(1)} %reshape_squeeze.5) | copy-start | bytes 18436
  20.2 10.8 %copy-start.25 = (f32[6,3,1,512]{3,1,2,0:T(4,128)S(1)}, f32[6,3,1,512]{3,1,2,0:T(4,128)}, u32[]{:S(2)}) copy-start(f32[6,3,1,512]{3,1,2,0:T(4,128)} %copy.124) | copy-start | bytes 110596
  20.2 10.8 %copy-start.31 = (f32[1,6,512]{2,1,0:T(8,128)S(1)}, f32[1,6,512]{2,1,0:T(8,128)}, u32[]{:S(2)}) copy-start(f32[1,6,512]{2,1,0:T(8,128)} %copy.126) | copy-start | bytes 36868
  50.7 7.7 %copy-start = (f32[1,6,3,96,512]{4,3,2,1,0:T(8,128)S(1)}, f32[1,6,3,96,512]{4,3,2,1,0:T(8,128)}, u32[]{:S(2)}) copy-start(f32[1,6,3,96,512]{4,3,2,1,0:T(8,128)} %param.34) | copy-start | bytes 10616836
  93.4 98.7 %all-gather.6.cloned.1.call-start = ((), (), s32[]{:S(2)}) async-start(), calls=%async_computation.3 | async-start | bytes 1769472 | tf_op jit(solution)/shard_map/all_gather | solution.py:38
  215.7 34.1 %all-to-all-start = ((f32[32,17,288]{2,1,0:T(8,128)}), f32[32,17,288]{2,1,0:T(8,128)}, u32[]{:S(2)}, u32[]{:S(2)}) async-start(f32[32,17,288]{2,1,0:T(8,128)} %all_to_all.16), calls=%async_computation | async-start | bytes 2359296 | tf_op jit(solution)/shard_map/all_to_all | solution.py:121
  219.5 125.8 %all-reduce.8.cloned.1.call-start = ((), (), s32[]{:S(2)}) async-start(), calls=%async_computation.4 | async-start | bytes 3145728 | tf_op jit(solution)/shard_map/psum | solution.py:140
  260.8 10.7 %copy-start.41 = (f32[1,1,512]{2,1,0:T(1,128)S(1)}, f32[1,1,512]{2,1,0:T(1,128)}, u32[]{:S(2)}) copy-start(f32[1,1,512]{2,1,0:T(1,128)} %get-tuple-element.45) | copy-start | bytes 6148
  261.8 11.6 %copy-start.45 = (f32[96]{0:T(128)S(1)}, f32[96]{0:T(128)}, u32[]{:S(2)}) copy-start(f32[96]{0:T(128)} %multiply_select_fusion.1) | copy-start | bytes 1156
  285.6 72.4 %copy-start.18 = (f32[3,96,512]{2,1,0:T(8,128)S(1)}, f32[3,96,512]{2,1,0:T(8,128)}, u32[]{:S(2)}) copy-start(f32[3,96,512]{2,1,0:T(8,128)} %get-tuple-element.3) | copy-start | bytes 1769476
  285.6 97.0 %all-gather.8.cloned.1.call-start = ((), (), s32[]{:S(2)}) async-start(), calls=%async_computation.5 | async-start | bytes 1769472 | tf_op jit(solution)/shard_map/all_gather | solution.py:38
  358.0 26.5 %copy-start.33 = (s32[2048]{0:T(1024)S(1)}, s32[2048]{0:T(1024)}, u32[]{:S(2)}) copy-start(s32[2048]{0:T(1024)} %pad_clamp_fusion) | copy-start | bytes 24580
  384.4 5.4 copy-start.11
  393.8 18.5 %copy-start.1 = (f32[1,6,3,96,512]{4,3,2,1,0:T(8,128)S(1)}, f32[1,6,3,96,512]{4,3,2,1,0:T(8,128)}, u32[]{:S(2)}) copy-start(f32[1,6,3,96,512]{4,3,2,1,0:T(8,128)} %param.34) | copy-start | bytes 10616836
  396.3 34.1 %all-to-all-start.1 = ((f32[32,17,288]{2,1,0:T(8,128)}), f32[32,17,288]{2,1,0:T(8,128)}, u32[]{:S(2)}, u32[]{:S(2)}) async-start(f32[32,17,288]{2,1,0:T(8,128)} %all_to_all.19), calls=%async_computation.1 | async-start | bytes 2359296 | tf_op jit(solution)/shard_map/all_to_all | solution.py:121
  400.1 125.1 %all-reduce.10.cloned.1.call-start = ((), (), s32[]{:S(2)}) async-start(), calls=%async_computation.6 | async-start | bytes 3145728 | tf_op jit(solution)/shard_map/psum | solution.py:140
  440.8 10.5 %copy-start.40 = (f32[1,1,512]{2,1,0:T(1,128)S(1)}, f32[1,1,512]{2,1,0:T(1,128)}, u32[]{:S(2)}) copy-start(f32[1,1,512]{2,1,0:T(1,128)} %get-tuple-element.43) | copy-start | bytes 6148
  441.7 11.5 %copy-start.44 = (f32[96]{0:T(128)S(1)}, f32[96]{0:T(128)}, u32[]{:S(2)}) copy-start(f32[96]{0:T(128)} %multiply_select_fusion) | copy-start | bytes 1156
  465.5 97.0 %all-gather.10.cloned.1.call-start = ((), (), s32[]{:S(2)}) async-start(), calls=%async_computation.7 | async-start | bytes 1769472 | tf_op jit(solution)/shard_map/all_gather | solution.py:38
  537.9 26.5 %copy-start.34 = (s32[2048]{0:T(1024)S(1)}, s32[2048]{0:T(1024)}, u32[]{:S(2)}) copy-start(s32[2048]{0:T(1024)} %pad_clamp_fusion) | copy-start | bytes 24580
  (33 other events, 88.0 us)
Sparse Core Ops, SparseCore 0:
  9.6 31.8 all-gather.11
  93.5 61.2 all-reduce.5
  167.6 24.4 all-gather.5
  285.7 59.5 all-reduce.7
  358.1 24.4 all-gather.7
  465.6 59.5 all-reduce.9
  538.0 24.4 all-gather.9
where the time goes:
time: 587 us; the launch traced here: 578 us
  waiting for transfers between devices  279 us (48%)
  other arithmetic  122 us (21%)
  local copies, waits for them, and re-layouts  115 us (20%)
  matrix products  38 us (6%)
  between operations  15.2 us (3%)
  starting transfers between devices  9.15 us (2%)
    psum x3, waiting for transfers between devices, on_device(): summed = lax.psum(injection, 'line')  180 us
    all_gather x4, waiting for transfers between devices, gather_full(): return lax.all_gather(block, 'line', axis=1, tiled=True)  74.8 us
    dot_general x3, matrix products, on_device(): lax.dot_general(summed, inverse_block, (((1,), (1,)), ((), ())), precisio...  38 us
    scatter-add x3, other arithmetic, on_device(): injection.at[scenario_range, fault_local]  36.6 us
    scatter-add x3, other arithmetic, spread_ends(): return jnp.zeros((history.shape[1], node_count), jnp.float32).at[:, termi...  29.3 us
    all_to_all x2, waiting for transfers between devices, on_device(): lax.all_to_all(buffer, ('net', 'line'), split_axis=0, concat_axis=0, tile...  24.6 us
    reduce_sum x6, other arithmetic, on_device(): history = (jnp.sum(wave_now, axis=0) - jnp.sum(admits, axis=0)) * live_float  20.3 us
    gather x4, local copies, waits for them, and re-layouts, terminal_values(): picked = jnp.take(voltage, terminal.reshape(-1), axis=1)  18.5 us
  transfers between devices with their start and end apart: 9, of which 9 were waited for; matrix products, arithmetic and copies ran while one was open for 11% of the time, Pallas kernels for 0%

commit v1 on v0

--- a/solution.py
+++ b/solution.py
@@ -137,7 +137,8 @@
         injection = injection.at[scenario_range, fault_local].add(
             jnp.where(fault_here, -fault_conductance * fault_value, 0.0)
         )
-        summed = lax.psum(injection, "line")
+        mixed_arr = lax.all_gather(injection, axis_name="line")
+        summed = jnp.sum(mixed_arr, 0)
         voltage_rows = lax.dot_general(
             summed,
             inverse_block,

time: 587 us -> 764 us (1.30)
  waiting for transfers between devices: 279 us -> 439 us
  other arithmetic: 122 us -> 139 us
    all_gather x0 -> x3, waiting for transfers between devices: none -> 344 us  [on_device(): mixed_arr = lax.all_gather(injection, axis_name='line')]
    psum x3 -> x0, waiting for transfers between devices: 180 us -> none  [on_device(): summed = lax.psum(injection, 'line')]
    reduce_sum x0 -> x3, other arithmetic: none -> 18.3 us  [on_device(): summed = jnp.sum(mixed_arr, 0)]
  transfers between devices with their start and end apart: 9 -> 9, of which waited for: 9 -> 9; matrix products, arithmetic and copies ran while one was open for 11% -> 9% of each run, Pallas kernels for 0% -> 0%
where the time goes in v1:
time: 764 us; the launch traced here: 754 us
  waiting for transfers between devices  439 us (57%)
  other arithmetic  139 us (18%)
  local copies, waits for them, and re-layouts  116 us (15%)
  matrix products  35 us (5%)
  between operations  15.1 us (2%)
  starting transfers between devices  9.15 us (1%)
    all_gather x3, waiting for transfers between devices, on_device(): mixed_arr = lax.all_gather(injection, axis_name='line')  344 us
    all_gather x4, waiting for transfers between devices, gather_full(): return lax.all_gather(block, 'line', axis=1, tiled=True)  70.4 us
    scatter-add x3, other arithmetic, on_device(): injection.at[scenario_range, fault_local]  36.7 us
    dot_general x3, matrix products, on_device(): lax.dot_general(summed, inverse_block, (((1,), (1,)), ((), ())), precisio...  35 us
    scatter-add x3, other arithmetic, spread_ends(): return jnp.zeros((history.shape[1], node_count), jnp.float32).at[:, termi...  29.5 us
    all_to_all x2, waiting for transfers between devices, on_device(): lax.all_to_all(buffer, ('net', 'line'), split_axis=0, concat_axis=0, tile...  24.3 us
    reduce_sum x6, other arithmetic, on_device(): history = (jnp.sum(wave_now, axis=0) - jnp.sum(admits, axis=0)) * live_float  20.3 us
    gather x4, local copies, waits for them, and re-layouts, terminal_values(): picked = jnp.take(voltage, terminal.reshape(-1), axis=1)  18.6 us
  transfers between devices with their start and end apart: 9, of which 9 were waited for; matrix products, arithmetic and copies ran while one was open for 9% of the time, Pallas kernels for 0%

profile of v1, /device:TPU:0, one launch (start us, length us, event | category | flops | bytes accessed | tf_op | source)
XLA Modules:
  0.0 753.8 jit_solution(11891334055179664168)
XLA Ops:
  32.9 8.6 %all-gather.18.cloned.1.call-done = f32[1,96,4096]{1,2,0:T(8,128)} async-done(((f32[1,96,512]{1,2,0:T(8,128)}), f32[1,96,4096]{1,2,0:T(8,128)}) %all-gather.18.cloned.1.call-update) | async-done | bytes 1572880 | tf_op jit(solution)/shard_map/all_gather | solution.py:38
  45.1 5.6 gather_fusion.5
  64.7 10.5 %scatter_custom_fusion = f32[96,4096]{0,1:T(8,128)} fusion(s32[1536]{0:T(1024)} %fusion.32, f32[1536,96]{1,0:T(8,128)} %copy.74, f32[]{:T(128)} %constant.37.clone.1), kind=kCustom, calls=%fused_computation.47 | custom fusion | flops 147456 | bytes 1573376 | tf_op jit(solution)/shard_map/scatter-add | solution.py:33
  81.1 12.3 %scatter_fusion = f32[96,4096]{1,0:T(8,128)} fusion(f32[96,4096]{1,0:T(8,128)} %copy.75, s32[96]{0:T(128)S(1)} %fusion.36, f32[96]{0:T(128)} %get-tuple-element.9), kind=kCustom, calls=%fused_computation.10 | custom fusion | flops 96 | bytes 1920 | tf_op jit(solution)/shard_map/scatter-add | solution.py:137
  93.6 116.0 %all-gather.20.cloned.1.call-done = f32[768,4096]{1,0:T(8,128)} async-done(((f32[96,4096]{1,0:T(8,128)}), f32[768,4096]{1,0:T(8,128)}) %all-gather.20.cloned.1.call-update) | async-done | bytes 12582928 | tf_op jit(solution)/shard_map/all_gather | solution.py:140
  209.7 6.9 reduce_sum.125
  216.5 12.7 %fusion.4 = f32[96,512]{1,0:T(8,128)} fusion(f32[96,4096]{1,0:T(8,128)} %reduce_sum.125, f32[1,512,4096]{2,1,0:T(8,128)} %param.19), kind=kOutput, calls=%fused_computation.21 | convolution fusion | flops 2415919104 | bytes 10158080 | tf_op jit(solution)/shard_map/dot_general | solution.py:142
  236.2 16.6 %all-gather.12.cloned.1.call-done = f32[96,4096]{1,0:T(8,128)} async-done(((f32[96,512]{1,0:T(8,128)}), f32[96,4096]{1,0:T(8,128)}) %all-gather.12.cloned.1.call-update) | async-done | bytes 1572880 | tf_op jit(solution)/shard_map/all_gather | solution.py:38
  255.6 5.6 gather_fusion.6
  299.3 11.3 %all-to-all-done = f32[32,17,288]{2,1,0:T(8,128)} async-done(((f32[32,17,288]{2,1,0:T(8,128)}), f32[32,17,288]{2,1,0:T(8,128)}, u32[]{:S(2)}, u32[]{:S(2)}) %all-to-all-start) | async-done | bytes 626720 | tf_op jit(solution)/shard_map/all_to_all | solution.py:121
  321.7 9.6 %scatter_custom_fusion.3 = f32[96,4096]{0,1:T(8,128)S(1)} fusion(s32[1536]{0:T(1024)} %fusion.32, f32[1536,96]{1,0:T(8,128)} %copy.84, f32[]{:T(128)} %constant.37.clone.1), kind=kCustom, calls=%fused_computation.45 | custom fusion | flops 147456 | bytes 1573376 | tf_op jit(solution)/shard_map/scatter-add | solution.py:33
  333.3 12.2 %scatter_fusion.1 = f32[96,4096]{1,0:T(8,128)} fusion(f32[96,4096]{1,0:T(8,128)} %copy.85, s32[96]{0:T(128)S(1)} %fusion.36, f32[96]{0:T(128)S(1)} %copy-done.41), kind=kCustom, calls=%fused_computation.13 | custom fusion | flops 96 | bytes 1920 | tf_op jit(solution)/shard_map/scatter-add | solution.py:137
  346.0 114.1 %all-gather.22.cloned.1.call-done = f32[768,4096]{1,0:T(8,128)} async-done(((f32[96,4096]{1,0:T(8,128)}), f32[768,4096]{1,0:T(8,128)}) %all-gather.22.cloned.1.call-update) | async-done | bytes 12582928 | tf_op jit(solution)/shard_map/all_gather | solution.py:140
  460.1 5.7 reduce_sum.129
  465.8 11.2 %fusion.2 = f32[96,512]{1,0:T(8,128)} fusion(f32[96,4096]{1,0:T(8,128)S(1)} %reduce_sum.129, f32[1,512,4096]{2,1,0:T(8,128)} %param.19), kind=kOutput, calls=%fused_computation.19 | convolution fusion | flops 2415919104 | bytes 10158080 | tf_op jit(solution)/shard_map/dot_general | solution.py:142
  479.0 21.6 %all-gather.14.cloned.1.call-done = f32[96,4096]{1,0:T(8,128)} async-done(((f32[96,512]{1,0:T(8,128)}), f32[96,4096]{1,0:T(8,128)}) %all-gather.14.cloned.1.call-update) | async-done | bytes 1572880 | tf_op jit(solution)/shard_map/all_gather | solution.py:38
  530.4 4.8 add_reduce_fusion
  535.2 13.1 %all-to-all-done.1 = f32[32,17,288]{2,1,0:T(8,128)} async-done(((f32[32,17,288]{2,1,0:T(8,128)}), f32[32,17,288]{2,1,0:T(8,128)}, u32[]{:S(2)}, u32[]{:S(2)}) %all-to-all-start.1) | async-done | bytes 626720 | tf_op jit(solution)/shard_map/all_to_all | solution.py:121
  559.8 9.4 %scatter_custom_fusion.6 = f32[96,4096]{0,1:T(8,128)S(1)} fusion(s32[1536]{0:T(1024)} %fusion.32, f32[1536,96]{1,0:T(8,128)S(1)} %copy.94, f32[]{:T(128)} %constant.37.clone.1), kind=kCustom, calls=%fused_computation.43 | custom fusion | flops 147456 | bytes 1573376 | tf_op jit(solution)/shard_map/scatter-add | solution.py:33
  571.0 12.3 %scatter_fusion.2 = f32[96,4096]{1,0:T(8,128)} fusion(f32[96,4096]{1,0:T(8,128)} %copy.95, s32[96]{0:T(128)S(1)} %fusion.36, f32[96]{0:T(128)S(1)} %copy-done.40), kind=kCustom, calls=%fused_computation.16 | custom fusion | flops 96 | bytes 1920 | tf_op jit(solution)/shard_map/scatter-add | solution.py:137
  583.6 114.3 %all-gather.24.cloned.1.call-done = f32[768,4096]{1,0:T(8,128)} async-done(((f32[96,4096]{1,0:T(8,128)}), f32[768,4096]{1,0:T(8,128)}) %all-gather.24.cloned.1.call-update) | async-done | bytes 12582928 | tf_op jit(solution)/shard_map/all_gather | solution.py:140
  697.9 5.7 reduce_sum.132
  703.6 11.2 %fusion = f32[96,512]{1,0:T(8,128)} fusion(f32[96,4096]{1,0:T(8,128)S(1)} %reduce_sum.132, f32[1,512,4096]{2,1,0:T(8,128)} %param.19), kind=kOutput, calls=%fused_computation.17 | convolution fusion | flops 2415919104 | bytes 10158080 | tf_op jit(solution)/shard_map/dot_general | solution.py:142
  714.8 23.6 %all-gather.16.cloned.1.call-done = f32[96,4096]{1,0:T(8,128)} async-done(((f32[96,512]{1,0:T(8,128)}), f32[96,4096]{1,0:T(8,128)}) %all-gather.16.cloned.1.call-update) | async-done | bytes 1572880 | tf_op jit(solution)/shard_map/all_gather | solution.py:38
  (210 shorter events, 163.8 us)
Async XLA Ops:
  7.2 18.6 %copy-start.42 = (s32[96]{0:T(128)S(1)}, s32[96]{0:T(128)}, u32[]{:S(2)}) copy-start(s32[96]{0:T(128)} %param.22) | copy-start | bytes 1156
  7.2 23.9 %copy-start.2 = (f32[1,6,3,96,512]{4,3,2,1,0:T(8,128)S(1)}, f32[1,6,3,96,512]{4,3,2,1,0:T(8,128)}, u32[]{:S(2)}) copy-start(f32[1,6,3,96,512]{4,3,2,1,0:T(8,128)} %param.33) | copy-start | bytes 10616836
  7.2 34.3 %all-gather.18.cloned.1.call-start = ((), (), s32[]{:S(2)}) async-start(), calls=%async_computation.5 | async-start | bytes 2359296 | tf_op jit(solution)/shard_map/all_gather | solution.py:38
  9.2 200.5 %all-gather.20.cloned.1.call-start = ((), (), s32[]{:S(2)}) async-start(), calls=%async_computation.6 | async-start | bytes 14155776 | tf_op jit(solution)/shard_map/all_gather | solution.py:140
  12.5 11.2 %copy-start.30 = (s32[1536]{0:T(1024)}, s32[1536]{0:T(1024)S(1)}, u32[]{:S(2)}) copy-start(s32[1536]{0:T(1024)S(1)} %reshape_squeeze.5) | copy-start | bytes 18436
  20.3 10.7 %copy-start.20 = (f32[6,3,1,512]{3,1,2,0:T(4,128)S(1)}, f32[6,3,1,512]{3,1,2,0:T(4,128)}, u32[]{:S(2)}) copy-start(f32[6,3,1,512]{3,1,2,0:T(4,128)} %copy.124) | copy-start | bytes 110596
  20.3 10.7 %copy-start.26 = (f32[1,6,512]{2,1,0:T(8,128)S(1)}, f32[1,6,512]{2,1,0:T(8,128)}, u32[]{:S(2)}) copy-start(f32[1,6,512]{2,1,0:T(8,128)} %copy.126) | copy-start | bytes 36868
  50.7 7.7 %copy-start = (f32[1,6,3,96,512]{4,3,2,1,0:T(8,128)S(1)}, f32[1,6,3,96,512]{4,3,2,1,0:T(8,128)}, u32[]{:S(2)}) copy-start(f32[1,6,3,96,512]{4,3,2,1,0:T(8,128)} %param.34) | copy-start | bytes 10616836
  93.4 159.4 %all-gather.12.cloned.1.call-start = ((), (), s32[]{:S(2)}) async-start(), calls=%async_computation.2 | async-start | bytes 1769472 | tf_op jit(solution)/shard_map/all_gather | solution.py:38
  276.4 34.1 %all-to-all-start = ((f32[32,17,288]{2,1,0:T(8,128)}), f32[32,17,288]{2,1,0:T(8,128)}, u32[]{:S(2)}, u32[]{:S(2)}) async-start(f32[32,17,288]{2,1,0:T(8,128)} %all_to_all.16), calls=%async_computation | async-start | bytes 2359296 | tf_op jit(solution)/shard_map/all_to_all | solution.py:121
  280.3 179.8 %all-gather.22.cloned.1.call-start = ((), (), s32[]{:S(2)}) async-start(), calls=%async_computation.7 | async-start | bytes 14155776 | tf_op jit(solution)/shard_map/all_gather | solution.py:140
  320.4 11.0 %copy-start.37 = (f32[1,1,512]{2,1,0:T(1,128)S(1)}, f32[1,1,512]{2,1,0:T(1,128)}, u32[]{:S(2)}) copy-start(f32[1,1,512]{2,1,0:T(1,128)} %get-tuple-element.45) | copy-start | bytes 6148
  320.6 12.7 %copy-start.41 = (f32[96]{0:T(128)S(1)}, f32[96]{0:T(128)}, u32[]{:S(2)}) copy-start(f32[96]{0:T(128)} %multiply_select_fusion.1) | copy-start | bytes 1156
  345.5 155.1 %all-gather.14.cloned.1.call-start = ((), (), s32[]{:S(2)}) async-start(), calls=%async_computation.3 | async-start | bytes 1769472 | tf_op jit(solution)/shard_map/all_gather | solution.py:38
  477.0 25.5 %copy-start.28 = (s32[2048]{0:T(1024)S(1)}, s32[2048]{0:T(1024)}, u32[]{:S(2)}) copy-start(s32[2048]{0:T(1024)} %pad_clamp_fusion) | copy-start | bytes 24580
  511.7 18.6 %copy-start.1 = (f32[1,6,3,96,512]{4,3,2,1,0:T(8,128)S(1)}, f32[1,6,3,96,512]{4,3,2,1,0:T(8,128)}, u32[]{:S(2)}) copy-start(f32[1,6,3,96,512]{4,3,2,1,0:T(8,128)} %param.34) | copy-start | bytes 10616836
  514.2 34.1 %all-to-all-start.1 = ((f32[32,17,288]{2,1,0:T(8,128)}), f32[32,17,288]{2,1,0:T(8,128)}, u32[]{:S(2)}, u32[]{:S(2)}) async-start(f32[32,17,288]{2,1,0:T(8,128)} %all_to_all.19), calls=%async_computation.1 | async-start | bytes 2359296 | tf_op jit(solution)/shard_map/all_to_all | solution.py:121
  518.0 179.8 %all-gather.24.cloned.1.call-start = ((), (), s32[]{:S(2)}) async-start(), calls=%async_computation.8 | async-start | bytes 14155776 | tf_op jit(solution)/shard_map/all_gather | solution.py:140
  530.4 19.3 %copy-start.34 = (s32[1024]{0:T(1024)S(1)}, s32[1024]{0:T(1024)}, u32[]{:S(2)}) copy-start(s32[1024]{0:T(1024)} %pad_clamp_fusion.1) | copy-start | bytes 12292
  558.6 10.5 %copy-start.36 = (f32[1,1,512]{2,1,0:T(1,128)S(1)}, f32[1,1,512]{2,1,0:T(1,128)}, u32[]{:S(2)}) copy-start(f32[1,1,512]{2,1,0:T(1,128)} %get-tuple-element.43) | copy-start | bytes 6148
  559.5 11.5 %copy-start.40 = (f32[96]{0:T(128)S(1)}, f32[96]{0:T(128)}, u32[]{:S(2)}) copy-start(f32[96]{0:T(128)} %multiply_select_fusion) | copy-start | bytes 1156
  583.3 155.1 %all-gather.16.cloned.1.call-start = ((), (), s32[]{:S(2)}) async-start(), calls=%async_computation.4 | async-start | bytes 1769472 | tf_op jit(solution)/shard_map/all_gather | solution.py:38
  714.8 25.5 %copy-start.29 = (s32[2048]{0:T(1024)S(1)}, s32[2048]{0:T(1024)}, u32[]{:S(2)}) copy-start(s32[2048]{0:T(1024)} %pad_clamp_fusion) | copy-start | bytes 24580
  740.3 5.4 copy-start.8
  (29 other events, 67.7 us)
Sparse Core Ops, SparseCore 0:
  9.6 31.8 all-gather.17
  93.5 116.0 all-gather.19
  229.3 23.4 all-gather.11
  345.6 114.3 all-gather.21
  477.1 23.4 all-gather.13
  583.4 114.3 all-gather.23
  714.9 23.4 all-gather.15
